TPU v7x, 32 devices: a whole 2x2x4 slice. The times are simulated.
32 devices in a mesh: group: 2 (over y), expert: 4 (over x, core), tensor: 4 (over z).
Axes of the slice: x: 2, y: 2, z: 4, core: 2. Of those that a mesh axis runs over, the one named last changes fastest.
Arguments:
- tokens: bfloat16 [512, 4096], P(('group', 'expert'), 'tensor'), parts along dimension 0, may hold values from -6 to 6
- w_gate: bfloat16 [8, 4096, 1536], P('expert', 'tensor'), may hold values from -0.125 to 0.125
- w_up: bfloat16 [8, 4096, 1536], P('expert', 'tensor'), may hold values from -0.125 to 0.125
- w_down: bfloat16 [8, 1536, 4096], P('expert', None, 'tensor'), may hold values from -0.15625 to 0.15625
- expert_ids: int32 [512, 8], P(('group', 'expert')), parts along dimension 0, may hold values from 0 to 7, as said below
- route_weights: float32 [512, 8], P(('group', 'expert')), parts along dimension 0, may hold values from 0.05 to 0.5
Outputs:
- mixed_out: bfloat16 [512, 4096], P(('group', 'expert'), 'tensor'), parts along dimension 0
There are 2 independent parts, one for each index of `group`. A program takes and returns all parts, laid end to end along the dimension named above; an argument that names none is the same for every part. Nothing has to cross between parts.
Inputs may be any that keep to these rules, and one draw needn't show every extreme that they name: `expert_ids`: each row names 8 different experts. In each aligned block of 64 rows no expert is named by more than 64 rows, and one expert, the same in every block of a part, is named by exactly 64 rows of every block.
All inputs are finite; a program needn't handle non-finite values.
Results may differ from a plain program's by a relative error of at most 0.0057.
Values may be sent and summed in bfloat16 or wider, within the bound.
A program may use at most 128 MiB of HBM per device.

v0:
```python
import functools

import jax
import jax.numpy as jnp
from jax import lax
from jax.experimental import pallas as pl
from jax.experimental.pallas import tpu as pltpu
from jax.sharding import PartitionSpec as P


def slot_numbers(flat_ids, experts_all):
    labels = jnp.arange(experts_all, dtype=jnp.int32)
    onehot = (flat_ids[:, None] == labels[None, :]).astype(jnp.int32)
    before = jnp.cumsum(onehot, axis=0) - onehot
    return jnp.sum(before * onehot, axis=1)


def routed_by_slots(tokens, w_gate, w_up, w_down, expert_ids, route_weights):
    n_expert = lax.axis_size("expert")
    held_experts = w_gate.shape[0]
    experts_all = held_experts * n_expert
    tok_rows = tokens.shape[0]
    col_share = tokens.shape[1]
    per_token = expert_ids.shape[1]
    capacity = min(tok_rows, 2 * tok_rows * per_token // experts_all)
    flat_ids = expert_ids.reshape(tok_rows * per_token)
    position = flat_ids * capacity + slot_numbers(flat_ids, experts_all)
    owners = jnp.arange(tok_rows * per_token, dtype=jnp.int32) // per_token
    source = jnp.full((experts_all * capacity,), -1, jnp.int32).at[position].set(owners)
    filled = (source >= 0)[:, None]
    picked_rows = jnp.where(filled, tokens[jnp.maximum(source, 0)], jnp.zeros((), tokens.dtype))
    outgoing = picked_rows.reshape(n_expert, held_experts, capacity, col_share)
    received = lax.all_to_all(outgoing, "expert", split_axis=0, concat_axis=0, tiled=True)
    gate_part = jnp.einsum("sjnd,jdf->sjnf", received, w_gate, preferred_element_type=jnp.float32)
    up_part = jnp.einsum("sjnd,jdf->sjnf", received, w_up, preferred_element_type=jnp.float32)
    gate_share = lax.psum_scatter(gate_part, "tensor", scatter_dimension=3, tiled=True)
    up_share = lax.psum_scatter(up_part, "tensor", scatter_dimension=3, tiled=True)
    hidden_share = (jax.nn.silu(gate_share) * up_share).astype(jnp.bfloat16)
    hidden = lax.all_gather(hidden_share, "tensor", axis=3, tiled=True)
    result = jnp.einsum("sjnf,jfd->sjnd", hidden, w_down, preferred_element_type=jnp.float32)
    returned = result.astype(jnp.bfloat16)
    combined = lax.all_to_all(returned, "expert", split_axis=0, concat_axis=0, tiled=True).reshape(
        experts_all * capacity, col_share
    )
    picked = combined[position].reshape(tok_rows, per_token, col_share).astype(jnp.float32)
    mixed_out = jnp.sum(picked * route_weights[:, :, None], axis=1)
    return mixed_out.astype(jnp.bfloat16)


LANES = 128
RS_LAG = 3
AG_LAG = 3
OUT_WIDTH = 256
MESH = pl.DeviceIdType.MESH


def layer_kernel(
    n_expert, n_tensor, tok_ref, ids_ref, weights_ref, wg_hbm, wu_hbm, wd_hbm, out_ref,
    rows_ref, route_ref, routes_ref, scale_ref, wg_ref, wu_ref, wd_ref, part_ref, sent_ref, got_ref, hidden_ref,
    acc_ref, pair_ref, far_out_ref, far_in_ref,
    w_sem, tok_send, tok_recv, pass_send, route_send, route_recv, rs_send, rs_recv, ag_send, ag_recv,
    pair_send, pair_recv, home_send, home_recv,
):
    held, depth, ff = wg_ref.shape
    tok_rows, cols = tok_ref.shape
    all_rows = n_expert * tok_rows
    per_expert = ff // LANES
    items = held * per_expert // 2
    me = lax.axis_index("expert")
    at = lax.axis_index("tensor")
    last = n_tensor - 1
    peers = [lax.rem(me + k, n_expert) for k in range(1, n_expert)]
    chips = n_expert // 2
    core = lax.rem(me, 2)
    chip = me // 2
    partner = 2 * chip + 1 - core
    same = [2 * lax.rem(chip + k, chips) + core for k in range(chips)]
    other = [2 * lax.rem(chip + k, chips) + 1 - core for k in range(chips)]

    loads = []
    for j in range(held):
        for k, (hbm, vmem) in enumerate(((wg_hbm, wg_ref), (wu_hbm, wu_ref))):
            loads.append(pltpu.make_async_copy(hbm.at[j], vmem.at[j], w_sem.at[2 * j + k]))
    loads.append(pltpu.make_async_copy(wd_hbm, wd_ref, w_sem.at[2 * held]))
    for load in loads:
        load.start()

    barrier = pltpu.get_barrier_semaphore()
    for peer in peers:
        pl.semaphore_signal(barrier, inc=1, device_id={"expert": peer}, device_id_type=MESH)

    @pl.when(at > 0)
    def _():
        pl.semaphore_signal(barrier, inc=1, device_id={"tensor": at - 1}, device_id_type=MESH)

    @pl.when(at < last)
    def _():
        pl.semaphore_signal(barrier, inc=1, device_id={"tensor": at + 1}, device_id_type=MESH)

    greeted = (n_expert - 1) + (at > 0).astype(jnp.int32) + (at < last).astype(jnp.int32)
    pl.semaphore_wait(barrier, greeted)

    def tok_copy(k, slot):
        return pltpu.make_async_remote_copy(
            src_ref=tok_ref, dst_ref=rows_ref.at[slot], send_sem=tok_send.at[k], recv_sem=tok_recv.at[slot],
            device_id={"expert": same[k] if k else partner}, device_id_type=MESH)

    def pass_copy(k, slot):
        return pltpu.make_async_remote_copy(
            src_ref=rows_ref.at[slot], dst_ref=rows_ref.at[slot], send_sem=pass_send.at[k],
            recv_sem=tok_recv.at[slot], device_id={"expert": partner}, device_id_type=MESH)

    def route_copy(k, slot):
        return pltpu.make_async_remote_copy(
            src_ref=route_ref, dst_ref=routes_ref.at[slot], send_sem=route_send.at[k], recv_sem=route_recv.at[slot],
            device_id={"expert": peers[k]}, device_id_type=MESH)

    for k in range(chips - 1, -1, -1):
        tok_copy(k, me).start()
    rows_ref[me] = tok_ref[...]
    labels = lax.broadcasted_iota(jnp.int32, (tok_rows, LANES), 1)
    routes = jnp.zeros((tok_rows, LANES), jnp.float32)
    for k in range(ids_ref.shape[1]):
        routes += jnp.where(ids_ref[:, k:k + 1] == labels, weights_ref[:, k:k + 1], 0.0)
    route_ref[...] = routes
    routes_ref[me] = routes
    for k in range(1, chips):
        tok_copy(k, same[k]).wait_recv()
        pass_copy(k, same[k]).start()
    for k in range(n_expert - 1):
        route_copy(k, me).start()
    for load in loads[:-1]:
        load.wait()
    tok_copy(0, partner).wait_recv()
    for k in range(1, chips):
        pass_copy(k, other[k]).wait_recv()

    far = (last - at, at)
    onward = (jnp.maximum(at - 1, 0), jnp.minimum(at + 1, last))
    back = (jnp.minimum(at + 1, last), jnp.maximum(at - 1, 0))

    def rs_copy(f, i):
        return pltpu.make_async_remote_copy(
            src_ref=sent_ref.at[f, i], dst_ref=got_ref.at[f, i], send_sem=rs_send.at[f, i], recv_sem=rs_recv.at[f, i],
            device_id={"tensor": onward[f]}, device_id_type=MESH)

    def ag_copy(f, i):
        return pltpu.make_async_remote_copy(
            src_ref=hidden_ref.at[f, i], dst_ref=hidden_ref.at[f, i], send_sem=ag_send.at[f, i],
            recv_sem=ag_recv.at[f, i], device_id={"tensor": back[f]}, device_id_type=MESH)

    def compute_part(f, i):
        q = f * items + i
        j = q // per_expert
        start = pl.multiple_of(lax.rem(q, per_expert) * LANES, LANES)
        both = jnp.concatenate([wg_ref[j, :, pl.ds(start, LANES)], wu_ref[j, :, pl.ds(start, LANES)]], axis=1)
        part_ref[f] = jnp.dot(rows_ref[...].reshape(all_rows, depth), both, preferred_element_type=jnp.float32)

    def finish_part(f, i):
        @pl.when(far[f] > 0)
        def _():
            rs_copy(f, i).wait_recv()
            part_ref[f] = part_ref[f] + got_ref[f, i].astype(jnp.float32)

        @pl.when(far[f] < last)
        def _():
            sent_ref[f, i] = part_ref[f].astype(jnp.bfloat16)
            rs_copy(f, i).start()

        @pl.when(far[f] == last)
        def _():
            gate = part_ref[f, :, :LANES]
            up = part_ref[f, :, LANES:]
            j = (f * items + i) // per_expert
            hidden_ref[f, i] = (jax.nn.silu(gate) * up * scale_ref[j]).astype(jnp.bfloat16)
            ag_copy(f, i).start()

    def step(s, carry):
        for f in range(2):
            i = s - RS_LAG * far[f]

            @pl.when((i >= 0) & (i < items))
            def _():
                compute_part(f, i)

        for f in range(2):
            i = s - RS_LAG * far[f]

            @pl.when((i >= 0) & (i < items))
            def _():
                finish_part(f, i)

        return carry

    lax.fori_loop(0, RS_LAG * last, step, 0)

    for k in range(n_expert - 1):
        route_copy(k, peers[k]).wait_recv()
    all_routes = routes_ref[...].reshape(all_rows, LANES)
    lane = lax.broadcasted_iota(jnp.int32, (all_rows, LANES), 1)
    for j in range(held):
        mine = jnp.sum(jnp.where(lane == me * held + j, all_routes, 0.0), axis=1, keepdims=True)
        scale_ref[j] = jnp.broadcast_to(mine, (all_rows, LANES))

    lax.fori_loop(RS_LAG * last, items + RS_LAG * last, step, 0)

    loads[-1].wait()
    acc_ref[...] = jnp.zeros_like(acc_ref)

    def collect(s, carry):
        for f in range(2):
            i = s - AG_LAG * (last - far[f])

            @pl.when((i >= 0) & (i < items) & (far[f] < last))
            def _():
                ag_copy(f, i).wait_recv()

                @pl.when(far[f] > 0)
                def _():
                    ag_copy(f, i).start()

        for f in range(2):
            i = s - AG_LAG * (last - far[f])

            @pl.when((i >= 0) & (i < items) & (lax.rem(i + items, 2) == 1))
            def _():
                q = f * items + i - 1
                j = q // per_expert
                start = pl.multiple_of(lax.rem(q, per_expert) * LANES, LANES)
                pair = jnp.concatenate([hidden_ref[f, i - 1], hidden_ref[f, i]], axis=1)
                for c in range(0, cols, OUT_WIDTH):
                    down = wd_ref[j, pl.ds(start, 2 * LANES), c:c + OUT_WIDTH]
                    term = jnp.dot(pair, down, preferred_element_type=jnp.float32)
                    acc_ref[:, :, c:c + OUT_WIDTH] += term.reshape(n_expert, tok_rows, OUT_WIDTH)

        return carry

    lax.fori_loop(0, items + AG_LAG * last, collect, 0)

    def pair_copy(k):
        return pltpu.make_async_remote_copy(
            src_ref=acc_ref.at[other[k]], dst_ref=pair_ref.at[k], send_sem=pair_send.at[k],
            recv_sem=pair_recv.at[k], device_id={"expert": partner}, device_id_type=MESH)

    def home_copy(k):
        return pltpu.make_async_remote_copy(
            src_ref=far_out_ref.at[k], dst_ref=far_in_ref.at[k], send_sem=home_send.at[k],
            recv_sem=home_recv.at[k], device_id={"expert": same[k]}, device_id_type=MESH)

    for k in range(chips - 1, -1, -1):
        pair_copy(k).start()
    for k in range(1, chips):
        pair_copy(k).wait_recv()
        far_out_ref[k] = (acc_ref[same[k]] + pair_ref[k]).astype(jnp.bfloat16)
        home_copy(k).start()

    for k in range(chips):
        tok_copy(k, me).wait_send()
        pair_copy(k).wait_send()
        if k:
            pass_copy(k, same[k]).wait_send()
    for k in range(n_expert - 1):
        route_copy(k, me).wait_send()

    def drain(i, carry):
        for f in range(2):
            @pl.when(far[f] < last)
            def _():
                rs_copy(f, i).wait_send()

            @pl.when(far[f] > 0)
            def _():
                ag_copy(f, i).wait_send()

        return carry

    lax.fori_loop(0, items, drain, 0)

    pair_copy(0).wait_recv()
    acc_ref[me] += pair_ref[0]
    total = acc_ref[me]
    for k in range(1, chips):
        home_copy(k).wait_recv()
        total = total + far_in_ref[k].astype(jnp.float32)
    out_ref[...] = total.astype(jnp.bfloat16)
    for k in range(1, chips):
        home_copy(k).wait_send()


def every_expert(tokens, w_gate, w_up, w_down, expert_ids, route_weights):
    n_expert = lax.axis_size("expert")
    n_tensor = lax.axis_size("tensor")
    held, depth, ff = w_gate.shape
    tok_rows, cols = tokens.shape
    all_rows = n_expert * tok_rows
    items = held * (ff // LANES) // 2
    chips = n_expert // 2
    dma = pltpu.SemaphoreType.DMA
    vmem = pl.BlockSpec(memory_space=pltpu.VMEM)
    hbm = pl.BlockSpec(memory_space=pl.ANY)
    bf16 = jnp.bfloat16
    return pl.pallas_call(
        functools.partial(layer_kernel, n_expert, n_tensor),
        out_shape=jax.ShapeDtypeStruct((tok_rows, cols), bf16),
        in_specs=[vmem, vmem, vmem, hbm, hbm, hbm],
        out_specs=vmem,
        scratch_shapes=[
            pltpu.VMEM((n_expert, tok_rows, cols), bf16),
            pltpu.VMEM((tok_rows, LANES), jnp.float32),
            pltpu.VMEM((n_expert, tok_rows, LANES), jnp.float32),
            pltpu.VMEM((held, all_rows, LANES), jnp.float32),
            pltpu.VMEM(w_gate.shape, bf16),
            pltpu.VMEM(w_up.shape, bf16),
            pltpu.VMEM(w_down.shape, bf16),
            pltpu.VMEM((2, all_rows, 2 * LANES), jnp.float32),
            pltpu.VMEM((2, items, all_rows, 2 * LANES), bf16),
            pltpu.VMEM((2, items, all_rows, 2 * LANES), bf16),
            pltpu.VMEM((2, items, all_rows, LANES), bf16),
            pltpu.VMEM((n_expert, tok_rows, cols), jnp.float32),
            pltpu.VMEM((chips, tok_rows, cols), jnp.float32),
            pltpu.VMEM((chips, tok_rows, cols), bf16),
            pltpu.VMEM((chips, tok_rows, cols), bf16),
            dma((2 * held + 1,)),
            dma((chips,)),
            dma((n_expert,)),
            dma((chips,)),
            dma((n_expert - 1,)),
            dma((n_expert,)),
            dma((2, items)),
            dma((2, items)),
            dma((2, items)),
            dma((2, items)),
            dma((chips,)),
            dma((chips,)),
            dma((chips,)),
            dma((chips,)),
        ],
        compiler_params=pltpu.CompilerParams(
            collective_id=0, has_side_effects=True, vmem_limit_bytes=56 * 1024 * 1024
        ),
    )(tokens, expert_ids, route_weights, w_gate, w_up, w_down)


def per_device(tokens, w_gate, w_up, w_down, expert_ids, route_weights):
    experts_all = w_gate.shape[0] * lax.axis_size("expert")
    if expert_ids.shape[1] == experts_all:
        return every_expert(tokens, w_gate, w_up, w_down, expert_ids, route_weights)
    return routed_by_slots(tokens, w_gate, w_up, w_down, expert_ids, route_weights)


def solution(mesh):
    in_specs = (
        P(("group", "expert"), "tensor"),
        P("expert", "tensor", None),
        P("expert", "tensor", None),
        P("expert", None, "tensor"),
        P(("group", "expert"), None),
        P(("group", "expert"), None),
    )
    out_specs = P(("group", "expert"), "tensor")
    return jax.shard_map(
        per_device, mesh=mesh, in_specs=in_specs, out_specs=out_specs, check_vma=False
    )
```

profile of v0, /device:TPU:0, one launch (start us, length us, event | category | flops | bytes accessed | tf_op | source)
XLA Modules:
  0.0 88.8 jit_solution(12987218615558665671)
XLA Ops:
  0.0 1.4 %copy.7.ids_ref = s32[64,8]{1,0:T(8,128)} copy(s32[64,8]{0,1:T(8,128)} %param.10) | data formatting | bytes 4096 | tf_op args[4]
  1.4 1.4 %copy.8.weights_ref = f32[64,8]{1,0:T(8,128)} copy(f32[64,8]{0,1:T(8,128)} %param.11) | data formatting | bytes 4096 | tf_op args[5]
  2.8 84.4 %shard_map.64 = bf16[64,1024]{1,0:T(8,128)(2,1)} custom-call(bf16[64,1024]{1,0:T(8,128)(2,1)} %tok_ref.1, s32[64,8]{1,0:T(8,128)} %copy.7.ids_ref, f32[64,8]{1,0:T(8,128)} %copy.8.weights_ref, bf16[2,1024,1536]{2,1,0:T(8,128)(2,1)} %wg_hbm.1, bf16[2,1024,1536]{2,1,0:T(8,128)(2,1)} %wu_hbm.1, bf16[2,1536,1024]{2,1,0:T(8,128)(2,1)} %wd_hbm.1), custom_call_target="tpu_custom_call" | custom-call | tf_op jit(solution)/shard_map/pallas_call | solution.py:302
  87.2 1.6 %copy.10 = bf16[64,1024]{1,0:T(8,128)(2,1)} copy(bf16[64,1024]{1,0:T(8,128)(2,1)} %shard_map.64) | data formatting | bytes 262144
where the time goes:
time: 90.3 us; the launch traced here: 88.8 us
  Pallas kernels  84.4 us (93%)
  local copies, waits for them, and re-layouts  4.32 us (5%)
    pallas_call x1, Pallas kernels, every_expert(): pl.pallas_call(functools.partial(layer_kernel, n_expert, n_tensor), out_s...  84.4 us
    unnamed x3, local copies, waits for them, and re-layouts  4.32 us

commit v1 on v0

v1 whole, which is shorter than its diff:
```python
import functools

import jax
import jax.numpy as jnp
from jax import lax
from jax.experimental import pallas as pl
from jax.experimental.pallas import tpu as pltpu
from jax.sharding import PartitionSpec as P


def slot_numbers(flat_ids, experts_all):
    labels = jnp.arange(experts_all, dtype=jnp.int32)
    onehot = (flat_ids[:, None] == labels[None, :]).astype(jnp.int32)
    before = jnp.cumsum(onehot, axis=0) - onehot
    return jnp.sum(before * onehot, axis=1)


def routed_by_slots(tokens, w_gate, w_up, w_down, expert_ids, route_weights):
    n_expert = lax.axis_size("expert")
    held_experts = w_gate.shape[0]
    experts_all = held_experts * n_expert
    tok_rows = tokens.shape[0]
    col_share = tokens.shape[1]
    per_token = expert_ids.shape[1]
    capacity = min(tok_rows, 2 * tok_rows * per_token // experts_all)
    flat_ids = expert_ids.reshape(tok_rows * per_token)
    position = flat_ids * capacity + slot_numbers(flat_ids, experts_all)
    owners = jnp.arange(tok_rows * per_token, dtype=jnp.int32) // per_token
    source = jnp.full((experts_all * capacity,), -1, jnp.int32).at[position].set(owners)
    filled = (source >= 0)[:, None]
    picked_rows = jnp.where(filled, tokens[jnp.maximum(source, 0)], jnp.zeros((), tokens.dtype))
    outgoing = picked_rows.reshape(n_expert, held_experts, capacity, col_share)
    received = lax.all_to_all(outgoing, "expert", split_axis=0, concat_axis=0, tiled=True)
    gate_part = jnp.einsum("sjnd,jdf->sjnf", received, w_gate, preferred_element_type=jnp.float32)
    up_part = jnp.einsum("sjnd,jdf->sjnf", received, w_up, preferred_element_type=jnp.float32)
    gate_share = lax.psum_scatter(gate_part, "tensor", scatter_dimension=3, tiled=True)
    up_share = lax.psum_scatter(up_part, "tensor", scatter_dimension=3, tiled=True)
    hidden_share = (jax.nn.silu(gate_share) * up_share).astype(jnp.bfloat16)
    hidden = lax.all_gather(hidden_share, "tensor", axis=3, tiled=True)
    result = jnp.einsum("sjnf,jfd->sjnd", hidden, w_down, preferred_element_type=jnp.float32)
    returned = result.astype(jnp.bfloat16)
    combined = lax.all_to_all(returned, "expert", split_axis=0, concat_axis=0, tiled=True).reshape(
        experts_all * capacity, col_share
    )
    picked = combined[position].reshape(tok_rows, per_token, col_share).astype(jnp.float32)
    mixed_out = jnp.sum(picked * route_weights[:, :, None], axis=1)
    return mixed_out.astype(jnp.bfloat16)


LANES = 128
CHUNK = 256
RS_LAG = 2
AG_LAG = 2
HEAD_OWN = 3
HEAD_PARTNER = 2
OUT_WIDTH = 512
MESH = pl.DeviceIdType.MESH


def layer_kernel(
    n_expert, n_tensor, tok_hbm, ids_hbm, weights_hbm, wg_hbm, wu_hbm, wd_hbm, out_ref,
    rows_ref, ids_ref, weights_ref, route_ref, routes_ref, scale_ref, wg_ref, wu_ref, wd_ref, part_ref, sent_ref,
    got_ref, hidden_ref, acc_ref, pair_ref, far_out_ref, far_in_ref,
    in_sem, w_sem, wd_sem, tok_send, tok_recv, pass_send, route_send, route_recv, rs_send, rs_recv, ag_send, ag_recv,
    pair_send, pair_recv, home_send, home_recv,
):
    held, depth, ff = wg_hbm.shape
    tok_rows, cols = tok_hbm.shape
    all_rows = n_expert * tok_rows
    per_expert = ff // CHUNK
    half = held * per_expert // 2
    items = n_expert * half
    me = lax.axis_index("expert")
    at = lax.axis_index("tensor")
    last = n_tensor - 1
    peers = [lax.rem(me + k, n_expert) for k in range(1, n_expert)]
    chips = n_expert // 2
    core = lax.rem(me, 2)
    chip = me // 2
    partner = 2 * chip + 1 - core
    same = [2 * lax.rem(chip + k, chips) + core for k in range(chips)]
    other = [2 * lax.rem(chip + k, chips) + 1 - core for k in range(chips)]

    segments = [(me, 0, HEAD_OWN), (partner, 0, HEAD_PARTNER)]
    for k in range(1, chips):
        segments += [(same[k], 0, half), (other[k], 0, half)]
    segments += [(partner, HEAD_PARTNER, half - HEAD_PARTNER), (me, HEAD_OWN, half - HEAD_OWN)]
    starts = [sum(count for _, _, count in segments[:n]) for n in range(len(segments))]
    ends = [start + segment[2] - 1 for start, segment in zip(starts, segments)]

    def item(i):
        block, chunk = me, i
        for start, (owner, first, _) in list(zip(starts, segments))[1:]:
            past = i >= start
            block = jnp.where(past, owner, block)
            chunk = jnp.where(past, i - start + first, chunk)
        return block, chunk

    def place(f, c):
        q = f * half + c
        return q // per_expert, pl.multiple_of(lax.rem(q, per_expert) * CHUNK, CHUNK)

    def w_copy(k, f, c):
        j, start = place(f, c)
        src = (wg_hbm, wu_hbm)[k].at[j, :, pl.ds(start, CHUNK)]
        return pltpu.make_async_copy(src, (wg_ref, wu_ref)[k].at[f, c], w_sem.at[k, f, c])

    def wd_copy(f, c):
        j, start = place(f, c)
        return pltpu.make_async_copy(wd_hbm.at[j, pl.ds(start, CHUNK), :], wd_ref.at[f, c], wd_sem.at[f, c])

    own_copies = [
        pltpu.make_async_copy(tok_hbm, rows_ref.at[me], in_sem.at[0]),
        pltpu.make_async_copy(ids_hbm, ids_ref, in_sem.at[1]),
        pltpu.make_async_copy(weights_hbm, weights_ref, in_sem.at[2]),
    ]
    for copy in own_copies:
        copy.start()
    for f in range(2):
        for k in range(2):
            w_copy(k, f, 0).start()

    barrier = pltpu.get_barrier_semaphore()
    for peer in peers:
        pl.semaphore_signal(barrier, inc=1, device_id={"expert": peer}, device_id_type=MESH)

    @pl.when(at > 0)
    def _():
        pl.semaphore_signal(barrier, inc=1, device_id={"tensor": at - 1}, device_id_type=MESH)

    @pl.when(at < last)
    def _():
        pl.semaphore_signal(barrier, inc=1, device_id={"tensor": at + 1}, device_id_type=MESH)

    for copy in own_copies:
        copy.wait()
    labels = lax.broadcasted_iota(jnp.int32, route_ref.shape, 0)
    routes = jnp.zeros(route_ref.shape, jnp.float32)
    for k in range(ids_ref.shape[0]):
        routes += jnp.where(ids_ref[k:k + 1, :] == labels, weights_ref[k:k + 1, :], 0.0)
    route_ref[...] = routes
    routes_ref[me] = routes

    greeted = (n_expert - 1) + (at > 0).astype(jnp.int32) + (at < last).astype(jnp.int32)
    pl.semaphore_wait(barrier, greeted)

    def tok_copy(k, slot):
        return pltpu.make_async_remote_copy(
            src_ref=rows_ref.at[slot], dst_ref=rows_ref.at[slot], send_sem=tok_send.at[k], recv_sem=tok_recv.at[slot],
            device_id={"expert": same[k] if k else partner}, device_id_type=MESH)

    def pass_copy(k, slot):
        return pltpu.make_async_remote_copy(
            src_ref=rows_ref.at[slot], dst_ref=rows_ref.at[slot], send_sem=pass_send.at[k],
            recv_sem=tok_recv.at[slot], device_id={"expert": partner}, device_id_type=MESH)

    def route_copy(k, slot):
        return pltpu.make_async_remote_copy(
            src_ref=route_ref, dst_ref=routes_ref.at[slot], send_sem=route_send.at[k], recv_sem=route_recv.at[slot],
            device_id={"expert": peers[k]}, device_id_type=MESH)

    for k in range(chips - 1, -1, -1):
        tok_copy(k, me).start()
    for k in range(n_expert - 1):
        route_copy(k, me).start()

    def load_rest(c, carry):
        for f in range(2):
            for k in range(2):
                w_copy(k, f, c).start()
        return carry

    lax.fori_loop(1, half, load_rest, 0)

    def load_down(c, carry):
        for f in range(2):
            wd_copy(f, c).start()
        return carry

    lax.fori_loop(0, half, load_down, 0)
    acc_ref[...] = jnp.zeros_like(acc_ref)

    def far_of(f):
        return jnp.where(f == 0, last - at, at)

    def onward(f):
        return jnp.where(f == 0, jnp.maximum(at - 1, 0), jnp.minimum(at + 1, last))

    def back(f):
        return jnp.where(f == 0, jnp.minimum(at + 1, last), jnp.maximum(at - 1, 0))

    near = jnp.where(at + at < n_tensor, 1, 0)
    order = (near, 1 - near)
    nearest = jnp.minimum(at, last - at)

    def rs_copy(f, i):
        return pltpu.make_async_remote_copy(
            src_ref=sent_ref.at[f, i], dst_ref=got_ref.at[f, i], send_sem=rs_send.at[f, i], recv_sem=rs_recv.at[f, i],
            device_id={"tensor": onward(f)}, device_id_type=MESH)

    def ag_copy(f, i):
        return pltpu.make_async_remote_copy(
            src_ref=hidden_ref.at[f, i], dst_ref=hidden_ref.at[f, i], send_sem=ag_send.at[f, i],
            recv_sem=ag_recv.at[f, i], device_id={"tensor": back(f)}, device_id_type=MESH)

    def wait_weights(c):
        for f in range(2):
            for k in range(2):
                w_copy(k, f, c).wait()

    def part_of_block(block, c):
        for f in range(2):
            for k, w_ref in enumerate((wg_ref, wu_ref)):
                part_ref[f, c, block, :, k * CHUNK:(k + 1) * CHUNK] = jnp.dot(
                    rows_ref[block], w_ref[f, c], preferred_element_type=jnp.float32)

    def part_of_all(c):
        for f in range(2):
            for k, w_ref in enumerate((wg_ref, wu_ref)):
                product = jnp.dot(
                    rows_ref[...].reshape(all_rows, depth), w_ref[f, c], preferred_element_type=jnp.float32)
                part_ref[f, c, :, :, k * CHUNK:(k + 1) * CHUNK] = product.reshape(n_expert, tok_rows, CHUNK)

    def prepare(i):
        @pl.when(i < HEAD_OWN)
        def _():
            wait_weights(i)

        @pl.when(i < HEAD_OWN + HEAD_PARTNER)
        def _():
            @pl.when(i == HEAD_OWN)
            def _():
                tok_copy(0, partner).wait_recv()

            block, c = item(i)
            part_of_block(block, c)

        @pl.when(i == HEAD_OWN + HEAD_PARTNER)
        def _():
            for k in range(1, chips):
                tok_copy(k, same[k]).wait_recv()
                pass_copy(k, same[k]).start()
            for k in range(1, chips):
                pass_copy(k, other[k]).wait_recv()

        @pl.when((i >= HEAD_OWN + HEAD_PARTNER) & (i < HEAD_OWN + HEAD_PARTNER + half))
        def _():
            c = i - (HEAD_OWN + HEAD_PARTNER)

            @pl.when(c >= HEAD_OWN)
            def _():
                wait_weights(c)

            part_of_all(c)

    def reduce_item(f, i):
        far = far_of(f)
        block, c = item(i)

        @pl.when(far == 0)
        def _():
            sent_ref[f, i] = part_ref[f, c, block].astype(jnp.bfloat16)

        @pl.when(far > 0)
        def _():
            rs_copy(f, i).wait_recv()

        @pl.when((far > 0) & (far < last))
        def _():
            sent_ref[f, i] = (part_ref[f, c, block] + got_ref[f, i].astype(jnp.float32)).astype(jnp.bfloat16)

        @pl.when(far < last)
        def _():
            rs_copy(f, i).start()

        @pl.when(far == last)
        def _():
            whole = part_ref[f, c, block] + got_ref[f, i].astype(jnp.float32)
            gate = whole[:, :CHUNK]
            up = whole[:, CHUNK:]
            j, _ = place(f, c)
            weight = jnp.concatenate([scale_ref[j, block]] * (CHUNK // LANES), axis=1)
            hidden_ref[f, i] = (jax.nn.silu(gate) * up * weight).astype(jnp.bfloat16)
            ag_copy(f, i).start()

    def scales():
        for k in range(n_expert - 1):
            route_copy(k, peers[k]).wait_recv()
        row = lax.broadcasted_iota(jnp.int32, (tok_rows, tok_rows), 0)
        column = lax.broadcasted_iota(jnp.int32, (tok_rows, tok_rows), 1)
        for j in range(held):
            for b in range(n_expert):
                mine = jnp.sum(
                    jnp.where(labels == me * held + j, routes_ref[b], 0.0), axis=0, keepdims=True)
                turned = jnp.sum(
                    jnp.where(row == column, jnp.broadcast_to(mine, (tok_rows, tok_rows)), 0.0), axis=1, keepdims=True)
                scale_ref[j, b] = jnp.broadcast_to(turned, (tok_rows, LANES))

    def wait_down(c, carry):
        for f in range(2):
            wd_copy(f, c).wait()
        return carry

    def down(f, i):
        block, c = item(i)
        for n in range(0, cols, OUT_WIDTH):
            acc_ref[block, :, n:n + OUT_WIDTH] += jnp.dot(
                hidden_ref[f, i], wd_ref[f, c, :, n:n + OUT_WIDTH], preferred_element_type=jnp.float32)

    def pair_copy():
        return pltpu.make_async_remote_copy(
            src_ref=acc_ref.at[partner], dst_ref=pair_ref, send_sem=pair_send,
            recv_sem=pair_recv, device_id={"expert": partner}, device_id_type=MESH)

    def home_copy(k, t):
        return pltpu.make_async_remote_copy(
            src_ref=far_out_ref.at[k, t], dst_ref=far_in_ref.at[k, t], send_sem=home_send.at[k, t],
            recv_sem=home_recv.at[k, t], device_id={"expert": (same, other)[t][k]}, device_id_type=MESH)

    turn = RS_LAG * last
    total = items + turn + AG_LAG * last

    def step(s, carry):
        for f in order:
            i = s - RS_LAG * far_of(f)

            @pl.when((i >= 0) & (i < items))
            def _():
                reduce_item(f, i)

        for f in order:
            far = far_of(f)
            i = s - turn - AG_LAG * (last - far)

            @pl.when((i >= 0) & (i < items) & (far < last))
            def _():
                ag_copy(f, i).wait_recv()

                @pl.when(far > 0)
                def _():
                    ag_copy(f, i).start()

        prepare(s + 1)

        @pl.when(s == turn - 1)
        def _():
            scales()
            lax.fori_loop(0, half, wait_down, 0)

        for f in order:
            i = s - turn - AG_LAG * (last - far_of(f))

            @pl.when((i >= 0) & (i < items))
            def _():
                down(f, i)

        done = s - turn - AG_LAG * (last - nearest)
        for k in range(1, chips):
            for t in range(2):
                @pl.when(done == ends[2 * k + t])
                def _():
                    far_out_ref[k, t] = acc_ref[(same, other)[t][k]].astype(jnp.bfloat16)
                    home_copy(k, t).start()

        @pl.when(done == ends[-2])
        def _():
            pair_copy().start()

        return carry

    prepare(0)
    lax.fori_loop(0, total, step, 0)

    pair_copy().wait_recv()
    result = acc_ref[me] + pair_ref[...]
    for k in range(1, chips):
        for t in range(2):
            home_copy(k, t).wait_recv()
            result = result + far_in_ref[k, t].astype(jnp.float32)
    out_ref[...] = result.astype(jnp.bfloat16)

    for k in range(chips):
        tok_copy(k, me).wait_send()
        if k:
            pass_copy(k, same[k]).wait_send()
            for t in range(2):
                home_copy(k, t).wait_send()
    pair_copy().wait_send()
    for k in range(n_expert - 1):
        route_copy(k, me).wait_send()

    def drain(i, carry):
        for f in range(2):
            @pl.when(far_of(f) < last)
            def _():
                rs_copy(f, i).wait_send()

            @pl.when(far_of(f) > 0)
            def _():
                ag_copy(f, i).wait_send()

        return carry

    lax.fori_loop(0, items, drain, 0)


def every_expert(tokens, w_gate, w_up, w_down, expert_ids, route_weights):
    n_expert = lax.axis_size("expert")
    n_tensor = lax.axis_size("tensor")
    held, depth, ff = w_gate.shape
    tok_rows, cols = tokens.shape
    experts_all = n_expert * held
    half = held * (ff // CHUNK) // 2
    items = n_expert * half
    chips = n_expert // 2
    dma = pltpu.SemaphoreType.DMA
    vmem = pl.BlockSpec(memory_space=pltpu.VMEM)
    hbm = pl.BlockSpec(memory_space=pl.ANY)
    bf16 = jnp.bfloat16
    f32 = jnp.float32
    per_token = expert_ids.shape[1]
    return pl.pallas_call(
        functools.partial(layer_kernel, n_expert, n_tensor),
        out_shape=jax.ShapeDtypeStruct((tok_rows, cols), bf16),
        in_specs=[hbm] * 6,
        out_specs=vmem,
        scratch_shapes=[
            pltpu.VMEM((n_expert, tok_rows, cols), bf16),
            pltpu.VMEM((per_token, tok_rows), jnp.int32),
            pltpu.VMEM((per_token, tok_rows), f32),
            pltpu.VMEM((experts_all, tok_rows), f32),
            pltpu.VMEM((n_expert, experts_all, tok_rows), f32),
            pltpu.VMEM((held, n_expert, tok_rows, LANES), f32),
            pltpu.VMEM((2, half, depth, CHUNK), bf16),
            pltpu.VMEM((2, half, depth, CHUNK), bf16),
            pltpu.VMEM((2, half, CHUNK, cols), bf16),
            pltpu.VMEM((2, half, n_expert, tok_rows, 2 * CHUNK), f32),
            pltpu.VMEM((2, items, tok_rows, 2 * CHUNK), bf16),
            pltpu.VMEM((2, items, tok_rows, 2 * CHUNK), bf16),
            pltpu.VMEM((2, items, tok_rows, CHUNK), bf16),
            pltpu.VMEM((n_expert, tok_rows, cols), f32),
            pltpu.VMEM((tok_rows, cols), f32),
            pltpu.VMEM((chips, 2, tok_rows, cols), bf16),
            pltpu.VMEM((chips, 2, tok_rows, cols), bf16),
            dma((3,)),
            dma((2, 2, half)),
            dma((2, half)),
            dma((chips,)),
            dma((n_expert,)),
            dma((chips,)),
            dma((n_expert - 1,)),
            dma((n_expert,)),
            dma((2, items)),
            dma((2, items)),
            dma((2, items)),
            dma((2, items)),
            dma,
            dma,
            dma((chips, 2)),
            dma((chips, 2)),
        ],
        compiler_params=pltpu.CompilerParams(
            collective_id=0, has_side_effects=True, vmem_limit_bytes=56 * 1024 * 1024
        ),
    )(tokens, expert_ids.T, route_weights.T, w_gate, w_up, w_down)


def per_device(tokens, w_gate, w_up, w_down, expert_ids, route_weights):
    experts_all = w_gate.shape[0] * lax.axis_size("expert")
    if expert_ids.shape[1] == experts_all:
        return every_expert(tokens, w_gate, w_up, w_down, expert_ids, route_weights)
    return routed_by_slots(tokens, w_gate, w_up, w_down, expert_ids, route_weights)


def solution(mesh):
    in_specs = (
        P(("group", "expert"), "tensor"),
        P("expert", "tensor", None),
        P("expert", "tensor", None),
        P("expert", None, "tensor"),
        P(("group", "expert"), None),
        P(("group", "expert"), None),
    )
    out_specs = P(("group", "expert"), "tensor")
    return jax.shard_map(
        per_device, mesh=mesh, in_specs=in_specs, out_specs=out_specs, check_vma=False
    )
```

time: 90.3 us -> 77 us (0.85); the launches traced: 88.8 us -> 76.8 us
  Pallas kernels: 84.4 us -> 75.3 us
  local copies, waits for them, and re-layouts: 4.32 us -> 1.57 us
    pallas_call x1, Pallas kernels: 84.4 us -> 75.3 us  [every_expert(): pl.pallas_call(functools.partial(layer_kernel, n_expert, n_tensor), out_s...]
    unnamed x3 -> x1, local copies, waits for them, and re-layouts: 4.32 us -> 1.57 us
where the time goes in v1:
time: 77 us; the launch traced here: 76.8 us
  Pallas kernels  75.3 us (98%)
  local copies, waits for them, and re-layouts  1.57 us (2%)
    pallas_call x1, Pallas kernels, every_expert(): pl.pallas_call(functools.partial(layer_kernel, n_expert, n_tensor), out_s...  75.3 us
    unnamed x1, local copies, waits for them, and re-layouts  1.57 us

profile of v1, /device:TPU:0, one launch (start us, length us, event | category | flops | bytes accessed | tf_op | source)
XLA Modules:
  0.0 76.8 jit_solution(7820647019485500286)
XLA Ops:
  0.0 75.3 %shard_map.64 = bf16[64,1024]{1,0:T(8,128)(2,1)} custom-call(bf16[64,1024]{1,0:T(8,128)(2,1)} %tok_hbm.1, s32[8,64]{1,0:T(8,128)} %bitcast.2, f32[8,64]{1,0:T(8,128)} %bitcast.3, bf16[2,1024,1536]{2,1,0:T(8,128)(2,1)} %wg_hbm.1, bf16[2,1024,1536]{2,1,0:T(8,128)(2,1)} %wu_hbm.1, bf16[2,1536,1024]{2,1,0:T(8,128)(2,1)} %wd_hbm.1), custom_call_target="tpu_custom_call" | custom-call | tf_op jit(solution)/shard_map/pallas_call | solution.py:422
  75.3 1.6 %copy.8 = bf16[64,1024]{1,0:T(8,128)(2,1)} copy(bf16[64,1024]{1,0:T(8,128)(2,1)} %shard_map.64) | data formatting | bytes 262144

commit v2 on v1

--- a/solution.py
+++ b/solution.py
@@ -49,8 +49,11 @@
 
 LANES = 128
 CHUNK = 256
-RS_LAG = 2
-AG_LAG = 2
+RS_HOP = 6
+AG_HOP = 5
+ALONE = 8
+HEAD_LOADS = 2
+SEND_LAG = 6
 HEAD_OWN = 3
 HEAD_PARTNER = 2
 OUT_WIDTH = 512
@@ -116,9 +119,10 @@
     ]
     for copy in own_copies:
         copy.start()
-    for f in range(2):
-        for k in range(2):
-            w_copy(k, f, 0).start()
+    for c in range(HEAD_LOADS):
+        for f in range(2):
+            for k in range(2):
+                w_copy(k, f, c).start()
 
     barrier = pltpu.get_barrier_semaphore()
     for peer in peers:
@@ -161,8 +165,6 @@
 
     for k in range(chips - 1, -1, -1):
         tok_copy(k, me).start()
-    for k in range(n_expert - 1):
-        route_copy(k, me).start()
 
     def load_rest(c, carry):
         for f in range(2):
@@ -170,15 +172,10 @@
                 w_copy(k, f, c).start()
         return carry
 
-    lax.fori_loop(1, half, load_rest, 0)
-
     def load_down(c, carry):
         for f in range(2):
             wd_copy(f, c).start()
         return carry
-
-    lax.fori_loop(0, half, load_down, 0)
-    acc_ref[...] = jnp.zeros_like(acc_ref)
 
     def far_of(f):
         return jnp.where(f == 0, last - at, at)
@@ -281,7 +278,6 @@
             j, _ = place(f, c)
             weight = jnp.concatenate([scale_ref[j, block]] * (CHUNK // LANES), axis=1)
             hidden_ref[f, i] = (jax.nn.silu(gate) * up * weight).astype(jnp.bfloat16)
-            ag_copy(f, i).start()
 
     def scales():
         for k in range(n_expert - 1):
@@ -317,50 +313,99 @@
             src_ref=far_out_ref.at[k, t], dst_ref=far_in_ref.at[k, t], send_sem=home_send.at[k, t],
             recv_sem=home_recv.at[k, t], device_id={"expert": (same, other)[t][k]}, device_id_type=MESH)
 
-    turn = RS_LAG * last
-    total = items + turn + AG_LAG * last
-
-    def step(s, carry):
+    turn = RS_HOP * last
+    mixed = 2 * ALONE
+    groups = (items - ALONE) // 2
+    after = mixed + 5 * groups
+    total = after + items - groups + AG_HOP * last
+
+    def reduce_at(t):
+        since = t - mixed
+        place_in = lax.rem(jnp.maximum(since, 0), 5)
+        early = (t >= 0) & (since < 0) & (lax.rem(jnp.maximum(t, 0), 2) == 0)
+        later = (since >= 0) & (t < after) & ((place_in == 0) | (place_in == 2))
+        i = jnp.where(since < 0, t // 2, ALONE + 2 * (since // 5) + place_in // 2)
+        return jnp.where(early | later, i, -1)
+
+    def gather_at(t):
+        since = t - mixed
+        beside = (since >= 0) & (t < after) & (lax.rem(jnp.maximum(since, 0), 5) == 4)
+        alone = (t >= after) & (t < after + items - groups)
+        i = jnp.where(t < after, since // 5, groups + t - after)
+        return jnp.where(beside | alone, i, -1)
+
+    def step(t, carry):
         for f in order:
-            i = s - RS_LAG * far_of(f)
-
-            @pl.when((i >= 0) & (i < items))
+            i = reduce_at(t - RS_HOP * far_of(f))
+
+            @pl.when(i >= 0)
             def _():
                 reduce_item(f, i)
 
         for f in order:
             far = far_of(f)
-            i = s - turn - AG_LAG * (last - far)
-
-            @pl.when((i >= 0) & (i < items) & (far < last))
-            def _():
-                ag_copy(f, i).wait_recv()
+            i = gather_at(t - AG_HOP * (last - far))
+
+            @pl.when(i >= 0)
+            def _():
+                @pl.when(far < last)
+                def _():
+                    ag_copy(f, i).wait_recv()
 
                 @pl.when(far > 0)
                 def _():
                     ag_copy(f, i).start()
 
-        prepare(s + 1)
-
-        @pl.when(s == turn - 1)
+        upcoming = reduce_at(t + 1)
+
+        @pl.when(upcoming > 0)
+        def _():
+            prepare(upcoming)
+
+        @pl.when(t == turn - 1)
         def _():
             scales()
             lax.fori_loop(0, half, wait_down, 0)
 
         for f in order:
-            i = s - turn - AG_LAG * (last - far_of(f))
-
-            @pl.when((i >= 0) & (i < items))
+            far = far_of(f)
+            i = jnp.where(far == last, reduce_at(t - turn), gather_at(t - AG_HOP * (last - far)))
+
+            @pl.when(i >= 0)
             def _():
                 down(f, i)
 
-        done = s - turn - AG_LAG * (last - nearest)
+        for f in order:
+            far = far_of(f)
+            i = gather_at(t - AG_HOP * (last - far))
+
+            @pl.when((i >= 0) & (far < last))
+            def _():
+                rs_copy(f, i).wait_send()
+
+            @pl.when((i >= SEND_LAG) & (far > 0))
+            def _():
+                ag_copy(f, i - SEND_LAG).wait_send()
+
+        done = gather_at(t - AG_HOP * (last - nearest))
+
+        @pl.when(t == 0)
+        def _():
+            for k in range(n_expert - 1):
+                route_copy(k, me).start()
+            lax.fori_loop(HEAD_LOADS, half, load_rest, 0)
+            acc_ref[...] = jnp.zeros_like(acc_ref)
+
+        @pl.when(t == 2 * HEAD_OWN)
+        def _():
+            lax.fori_loop(0, half, load_down, 0)
+
         for k in range(1, chips):
-            for t in range(2):
-                @pl.when(done == ends[2 * k + t])
+            for t_core in range(2):
+                @pl.when(done == ends[2 * k + t_core])
                 def _():
-                    far_out_ref[k, t] = acc_ref[(same, other)[t][k]].astype(jnp.bfloat16)
-                    home_copy(k, t).start()
+                    far_out_ref[k, t_core] = acc_ref[(same, other)[t_core][k]].astype(jnp.bfloat16)
+                    home_copy(k, t_core).start()
 
         @pl.when(done == ends[-2])
         def _():
@@ -391,17 +436,13 @@
 
     def drain(i, carry):
         for f in range(2):
-            @pl.when(far_of(f) < last)
-            def _():
-                rs_copy(f, i).wait_send()
-
             @pl.when(far_of(f) > 0)
             def _():
                 ag_copy(f, i).wait_send()
 
         return carry
 
-    lax.fori_loop(0, items, drain, 0)
+    lax.fori_loop(items - SEND_LAG, items, drain, 0)
 
 
 def every_expert(tokens, w_gate, w_up, w_down, expert_ids, route_weights):

time: 77 us -> 71.7 us (0.931)
  Pallas kernels: 75.3 us -> 70 us
    pallas_call x1, Pallas kernels: 75.3 us -> 70 us  [every_expert(): pl.pallas_call(functools.partial(layer_kernel, n_expert, n_tensor), out_s...]
where the time goes in v2:
time: 71.7 us; the launch traced here: 71.6 us
  Pallas kernels  70 us (98%)
  local copies, waits for them, and re-layouts  1.57 us (2%)
    pallas_call x1, Pallas kernels, every_expert(): pl.pallas_call(functools.partial(layer_kernel, n_expert, n_tensor), out_s...  70 us
    unnamed x1, local copies, waits for them, and re-layouts  1.57 us

profile of v2, /device:TPU:0, one launch (start us, length us, event | category | flops | bytes accessed | tf_op | source)
XLA Modules:
  0.0 71.6 jit_solution(15710764799506528801)
XLA Ops:
  0.0 70.0 %shard_map.64 = bf16[64,1024]{1,0:T(8,128)(2,1)} custom-call(bf16[64,1024]{1,0:T(8,128)(2,1)} %tok_hbm.1, s32[8,64]{1,0:T(8,128)} %bitcast.2, f32[8,64]{1,0:T(8,128)} %bitcast.3, bf16[2,1024,1536]{2,1,0:T(8,128)(2,1)} %wg_hbm.1, bf16[2,1024,1536]{2,1,0:T(8,128)(2,1)} %wu_hbm.1, bf16[2,1536,1024]{2,1,0:T(8,128)(2,1)} %wd_hbm.1), custom_call_target="tpu_custom_call" | custom-call | tf_op jit(solution)/shard_map/pallas_call | solution.py:463
  70.0 1.6 %copy.8 = bf16[64,1024]{1,0:T(8,128)(2,1)} copy(bf16[64,1024]{1,0:T(8,128)(2,1)} %shard_map.64) | data formatting | bytes 262144

commit v3 on v2

--- a/solution.py
+++ b/solution.py
@@ -50,10 +50,10 @@
 LANES = 128
 CHUNK = 256
 RS_HOP = 6
-AG_HOP = 5
+AG_HOP = 6
 ALONE = 8
-HEAD_LOADS = 2
-SEND_LAG = 6
+RS_SLOTS = 12
+AG_SLOTS = 20
 HEAD_OWN = 3
 HEAD_PARTNER = 2
 OUT_WIDTH = 512
@@ -62,7 +62,7 @@
 
 def layer_kernel(
     n_expert, n_tensor, tok_hbm, ids_hbm, weights_hbm, wg_hbm, wu_hbm, wd_hbm, out_ref,
-    rows_ref, ids_ref, weights_ref, route_ref, routes_ref, scale_ref, wg_ref, wu_ref, wd_ref, part_ref, sent_ref,
+    rows_ref, ids_ref, weights_ref, route_ref, routes_ref, scale_ref, w_ref, wd_ref, part_ref, sent_ref,
     got_ref, hidden_ref, acc_ref, pair_ref, far_out_ref, far_in_ref,
     in_sem, w_sem, wd_sem, tok_send, tok_recv, pass_send, route_send, route_recv, rs_send, rs_recv, ag_send, ag_recv,
     pair_send, pair_recv, home_send, home_recv,
@@ -106,11 +106,14 @@
     def w_copy(k, f, c):
         j, start = place(f, c)
         src = (wg_hbm, wu_hbm)[k].at[j, :, pl.ds(start, CHUNK)]
-        return pltpu.make_async_copy(src, (wg_ref, wu_ref)[k].at[f, c], w_sem.at[k, f, c])
-
-    def wd_copy(f, c):
-        j, start = place(f, c)
-        return pltpu.make_async_copy(wd_hbm.at[j, pl.ds(start, CHUNK), :], wd_ref.at[f, c], wd_sem.at[f, c])
+        return pltpu.make_async_copy(src, w_ref.at[c, f, k], w_sem.at[c])
+
+    def load_chunk(c):
+        for f in range(2):
+            for k in range(2):
+                w_copy(k, f, c).start()
+
+    load_down = pltpu.make_async_copy(wd_hbm, wd_ref, wd_sem)
 
     own_copies = [
         pltpu.make_async_copy(tok_hbm, rows_ref.at[me], in_sem.at[0]),
@@ -119,10 +122,7 @@
     ]
     for copy in own_copies:
         copy.start()
-    for c in range(HEAD_LOADS):
-        for f in range(2):
-            for k in range(2):
-                w_copy(k, f, c).start()
+    load_chunk(0)
 
     barrier = pltpu.get_barrier_semaphore()
     for peer in peers:
@@ -136,15 +136,7 @@
     def _():
         pl.semaphore_signal(barrier, inc=1, device_id={"tensor": at + 1}, device_id_type=MESH)
 
-    for copy in own_copies:
-        copy.wait()
-    labels = lax.broadcasted_iota(jnp.int32, route_ref.shape, 0)
-    routes = jnp.zeros(route_ref.shape, jnp.float32)
-    for k in range(ids_ref.shape[0]):
-        routes += jnp.where(ids_ref[k:k + 1, :] == labels, weights_ref[k:k + 1, :], 0.0)
-    route_ref[...] = routes
-    routes_ref[me] = routes
-
+    own_copies[0].wait()
     greeted = (n_expert - 1) + (at > 0).astype(jnp.int32) + (at < last).astype(jnp.int32)
     pl.semaphore_wait(barrier, greeted)
 
@@ -165,17 +157,24 @@
 
     for k in range(chips - 1, -1, -1):
         tok_copy(k, me).start()
+    load_chunk(1)
 
     def load_rest(c, carry):
-        for f in range(2):
-            for k in range(2):
-                w_copy(k, f, c).start()
+        load_chunk(c)
         return carry
 
-    def load_down(c, carry):
-        for f in range(2):
-            wd_copy(f, c).start()
-        return carry
+    def send_routes():
+        for copy in own_copies[1:]:
+            copy.wait()
+        routes = jnp.zeros(route_ref.shape, jnp.float32)
+        for k in range(ids_ref.shape[0]):
+            routes += jnp.where(ids_ref[k:k + 1, :] == labels, weights_ref[k:k + 1, :], 0.0)
+        route_ref[...] = routes
+        routes_ref[me] = routes
+        for k in range(n_expert - 1):
+            route_copy(k, me).start()
+
+    labels = lax.broadcasted_iota(jnp.int32, route_ref.shape, 0)
 
     def far_of(f):
         return jnp.where(f == 0, last - at, at)
@@ -192,30 +191,33 @@
 
     def rs_copy(f, i):
         return pltpu.make_async_remote_copy(
-            src_ref=sent_ref.at[f, i], dst_ref=got_ref.at[f, i], send_sem=rs_send.at[f, i], recv_sem=rs_recv.at[f, i],
-            device_id={"tensor": onward(f)}, device_id_type=MESH)
+            src_ref=sent_ref.at[f, i], dst_ref=got_ref.at[f, i], send_sem=rs_send.at[f],
+            recv_sem=rs_recv.at[f, lax.rem(i, RS_SLOTS)], device_id={"tensor": onward(f)}, device_id_type=MESH)
 
     def ag_copy(f, i):
         return pltpu.make_async_remote_copy(
-            src_ref=hidden_ref.at[f, i], dst_ref=hidden_ref.at[f, i], send_sem=ag_send.at[f, i],
-            recv_sem=ag_recv.at[f, i], device_id={"tensor": back(f)}, device_id_type=MESH)
+            src_ref=hidden_ref.at[f, i], dst_ref=hidden_ref.at[f, i], send_sem=ag_send.at[f],
+            recv_sem=ag_recv.at[f, lax.rem(i, AG_SLOTS)], device_id={"tensor": back(f)}, device_id_type=MESH)
+
+    def all_sent(ref, sem):
+        return pltpu.make_async_remote_copy(
+            src_ref=ref, dst_ref=ref, send_sem=sem, recv_sem=rs_recv.at[0, 0],
+            device_id={"tensor": onward(0)}, device_id_type=MESH)
 
     def wait_weights(c):
+        pltpu.make_async_copy(w_ref.at[c], w_ref.at[c], w_sem.at[c]).wait()
+
+    def part_of_block(block, c):
         for f in range(2):
             for k in range(2):
-                w_copy(k, f, c).wait()
-
-    def part_of_block(block, c):
-        for f in range(2):
-            for k, w_ref in enumerate((wg_ref, wu_ref)):
                 part_ref[f, c, block, :, k * CHUNK:(k + 1) * CHUNK] = jnp.dot(
-                    rows_ref[block], w_ref[f, c], preferred_element_type=jnp.float32)
+                    rows_ref[block], w_ref[c, f, k], preferred_element_type=jnp.float32)
 
     def part_of_all(c):
         for f in range(2):
-            for k, w_ref in enumerate((wg_ref, wu_ref)):
+            for k in range(2):
                 product = jnp.dot(
-                    rows_ref[...].reshape(all_rows, depth), w_ref[f, c], preferred_element_type=jnp.float32)
+                    rows_ref[...].reshape(all_rows, depth), w_ref[c, f, k], preferred_element_type=jnp.float32)
                 part_ref[f, c, :, :, k * CHUNK:(k + 1) * CHUNK] = product.reshape(n_expert, tok_rows, CHUNK)
 
     def prepare(i):
@@ -292,16 +294,12 @@
                     jnp.where(row == column, jnp.broadcast_to(mine, (tok_rows, tok_rows)), 0.0), axis=1, keepdims=True)
                 scale_ref[j, b] = jnp.broadcast_to(turned, (tok_rows, LANES))
 
-    def wait_down(c, carry):
-        for f in range(2):
-            wd_copy(f, c).wait()
-        return carry
-
     def down(f, i):
         block, c = item(i)
+        j, start = place(f, c)
         for n in range(0, cols, OUT_WIDTH):
             acc_ref[block, :, n:n + OUT_WIDTH] += jnp.dot(
-                hidden_ref[f, i], wd_ref[f, c, :, n:n + OUT_WIDTH], preferred_element_type=jnp.float32)
+                hidden_ref[f, i], wd_ref[j, pl.ds(start, CHUNK), n:n + OUT_WIDTH], preferred_element_type=jnp.float32)
 
     def pair_copy():
         return pltpu.make_async_remote_copy(
@@ -365,7 +363,7 @@
         @pl.when(t == turn - 1)
         def _():
             scales()
-            lax.fori_loop(0, half, wait_down, 0)
+            load_down.wait()
 
         for f in order:
             far = far_of(f)
@@ -375,30 +373,17 @@
             def _():
                 down(f, i)
 
-        for f in order:
-            far = far_of(f)
-            i = gather_at(t - AG_HOP * (last - far))
-
-            @pl.when((i >= 0) & (far < last))
-            def _():
-                rs_copy(f, i).wait_send()
-
-            @pl.when((i >= SEND_LAG) & (far > 0))
-            def _():
-                ag_copy(f, i - SEND_LAG).wait_send()
-
         done = gather_at(t - AG_HOP * (last - nearest))
 
         @pl.when(t == 0)
         def _():
-            for k in range(n_expert - 1):
-                route_copy(k, me).start()
-            lax.fori_loop(HEAD_LOADS, half, load_rest, 0)
+            lax.fori_loop(2, half, load_rest, 0)
+            send_routes()
             acc_ref[...] = jnp.zeros_like(acc_ref)
 
         @pl.when(t == 2 * HEAD_OWN)
         def _():
-            lax.fori_loop(0, half, load_down, 0)
+            load_down.start()
 
         for k in range(1, chips):
             for t_core in range(2):
@@ -434,15 +419,14 @@
     for k in range(n_expert - 1):
         route_copy(k, me).wait_send()
 
-    def drain(i, carry):
-        for f in range(2):
-            @pl.when(far_of(f) > 0)
-            def _():
-                ag_copy(f, i).wait_send()
-
-        return carry
-
-    lax.fori_loop(items - SEND_LAG, items, drain, 0)
+    for f in range(2):
+        @pl.when(far_of(f) < last)
+        def _():
+            all_sent(sent_ref.at[f], rs_send.at[f]).wait_send()
+
+        @pl.when(far_of(f) > 0)
+        def _():
+            all_sent(hidden_ref.at[f], ag_send.at[f]).wait_send()
 
 
 def every_expert(tokens, w_gate, w_up, w_down, expert_ids, route_weights):
@@ -472,9 +456,8 @@
             pltpu.VMEM((experts_all, tok_rows), f32),
             pltpu.VMEM((n_expert, experts_all, tok_rows), f32),
             pltpu.VMEM((held, n_expert, tok_rows, LANES), f32),
-            pltpu.VMEM((2, half, depth, CHUNK), bf16),
-            pltpu.VMEM((2, half, depth, CHUNK), bf16),
-            pltpu.VMEM((2, half, CHUNK, cols), bf16),
+            pltpu.VMEM((half, 2, 2, depth, CHUNK), bf16),
+            pltpu.VMEM(w_down.shape, bf16),
             pltpu.VMEM((2, half, n_expert, tok_rows, 2 * CHUNK), f32),
             pltpu.VMEM((2, items, tok_rows, 2 * CHUNK), bf16),
             pltpu.VMEM((2, items, tok_rows, 2 * CHUNK), bf16),
@@ -484,17 +467,17 @@
             pltpu.VMEM((chips, 2, tok_rows, cols), bf16),
             pltpu.VMEM((chips, 2, tok_rows, cols), bf16),
             dma((3,)),
-            dma((2, 2, half)),
-            dma((2, half)),
+            dma((half,)),
+            dma,
             dma((chips,)),
             dma((n_expert,)),
             dma((chips,)),
             dma((n_expert - 1,)),
             dma((n_expert,)),
-            dma((2, items)),
-            dma((2, items)),
-            dma((2, items)),
-            dma((2, items)),
+            dma((2,)),
+            dma((2, RS_SLOTS)),
+            dma((2,)),
+            dma((2, AG_SLOTS)),
             dma,
             dma,
             dma((chips, 2)),

time: 71.7 us -> 69.6 us (0.971)
  Pallas kernels: 70 us -> 67.9 us
    pallas_call x1, Pallas kernels: 70 us -> 67.9 us  [every_expert(): pl.pallas_call(functools.partial(layer_kernel, n_expert, n_tensor), out_s...]
where the time goes in v3:
time: 69.6 us; the launch traced here: 69.4 us
  Pallas kernels  67.9 us (98%)
  local copies, waits for them, and re-layouts  1.57 us (2%)
    pallas_call x1, Pallas kernels, every_expert(): pl.pallas_call(functools.partial(layer_kernel, n_expert, n_tensor), out_s...  67.9 us
    unnamed x1, local copies, waits for them, and re-layouts  1.57 us

profile of v3, /device:TPU:0, one launch (start us, length us, event | category | flops | bytes accessed | tf_op | source)
XLA Modules:
  0.0 69.4 jit_solution(8463284365006492176)
XLA Ops:
  0.0 67.9 %shard_map.64 = bf16[64,1024]{1,0:T(8,128)(2,1)} custom-call(bf16[64,1024]{1,0:T(8,128)(2,1)} %tok_hbm.1, s32[8,64]{1,0:T(8,128)} %bitcast.2, f32[8,64]{1,0:T(8,128)} %bitcast.3, bf16[2,1024,1536]{2,1,0:T(8,128)(2,1)} %wg_hbm.1, bf16[2,1024,1536]{2,1,0:T(8,128)(2,1)} %wu_hbm.1, bf16[2,1536,1024]{2,1,0:T(8,128)(2,1)} %wd_hbm.1), custom_call_target="tpu_custom_call" | custom-call | tf_op jit(solution)/shard_map/pallas_call | solution.py:447
  67.9 1.6 %copy.8 = bf16[64,1024]{1,0:T(8,128)(2,1)} copy(bf16[64,1024]{1,0:T(8,128)(2,1)} %shard_map.64) | data formatting | bytes 262144
